TPU v7x, 32 devices: a whole 2x2x4 slice. The times are simulated.
32 devices in a mesh: node: 4 (over z), local: 8 (over y, x, core).
Axes of the slice: x: 2, y: 2, z: 4, core: 2. Of those that a mesh axis runs over, the one named last changes fastest.
Arguments:
- tokens: bfloat16 [4096, 5120], P(('node', 'local')), may hold values from -6 to 6
- routes: int32 [4096, 6], P(('node', 'local')), may hold values from 0 to 31, all different within a row; in each aligned block of 128 rows (0 to 127, 128 to 255, ...) at most 32 rows name the same one
- route_weights: float32 [4096, 6], P(('node', 'local')), may hold values from 0.05 to 1
- w_gate: bfloat16 [32, 5120, 768], P(('node', 'local')), may hold values from -0.078125 to 0.078125
- w_up: bfloat16 [32, 5120, 768], P(('node', 'local')), may hold values from -0.078125 to 0.078125
- w_down: bfloat16 [32, 768, 5120], P(('node', 'local')), may hold values from -0.21875 to 0.21875
Outputs:
- mixed: bfloat16 [4096, 5120], P(('node', 'local'))
- balance_loss: float32 [], replicated
Inputs may be any that keep to these rules, and one draw needn't show every extreme that they name: `routes`: each row names 6 different experts. Among the rows of one device no expert is named more than 32 times, a bound that some block reaches.
All inputs are finite; a program needn't handle non-finite values.
Results may differ from a plain program's by a relative error of at most 0.0025.
The roundings to bfloat16 on the way count: a program that leaves them out, or rounds other values in their place, can miss the bound.
Values may be sent and summed in bfloat16 or wider, within the bound.
A program may use at most 128 MiB of HBM per device.

v0:
```python
import jax
import jax.numpy as jnp
from jax import lax
from jax.sharding import PartitionSpec as P

TOPK = 6


def expert_apply(rows, w_gate, w_up, w_down):
    gate = jnp.einsum("erd,edf->erf", rows, w_gate, preferred_element_type=jnp.float32)
    upper = jnp.einsum("erd,edf->erf", rows, w_up, preferred_element_type=jnp.float32)
    hidden = (jax.nn.silu(gate) * upper).astype(jnp.bfloat16)
    return jnp.einsum("erf,efd->erd", hidden, w_down, preferred_element_type=jnp.float32).astype(
        jnp.bfloat16
    )


def local(tokens, routes, route_weights, w_gate, w_up, w_down):
    n_node = lax.axis_size("node")
    n_local = lax.axis_size("local")
    exp_dev = w_gate.shape[0]
    devices = n_node * n_local
    experts = exp_dev * devices
    tok_dev = tokens.shape[0]
    width = tokens.shape[1]
    capacity = 4 * tok_dev * TOPK // (3 * experts)
    flat = routes.reshape(-1)
    labels = jnp.arange(experts, dtype=jnp.int32)
    onehot = (flat[:, None] == labels[None, :]).astype(jnp.int32)
    running = jnp.cumsum(onehot, axis=0) - onehot
    slots = jnp.sum(running * onehot, axis=1)
    position = flat * capacity + slots
    counts = jnp.sum(onehot, axis=0).astype(jnp.float32)
    weight_sums = jnp.sum(onehot.astype(jnp.float32) * route_weights.reshape(-1)[:, None], axis=0)
    counts_all, sums_all = lax.psum((counts, weight_sums), ("node", "local"))
    repeated = jnp.repeat(tokens, TOPK, axis=0)
    outgoing = jnp.zeros((experts * capacity, width), jnp.bfloat16).at[position].set(repeated)
    piece = lax.all_to_all(
        outgoing.reshape(experts, 1, capacity, width),
        ("node", "local"),
        split_axis=0,
        concat_axis=1,
        tiled=True,
    )
    held, sources, count, breadth = piece.shape
    rows = piece.reshape(held, sources * count, breadth)
    result = expert_apply(rows, w_gate, w_up, w_down)
    result = result.reshape(held, sources, count, breadth)
    returned = lax.all_to_all(result, ("node", "local"), split_axis=1, concat_axis=0, tiled=True)
    returned = returned.reshape(experts * capacity, width)
    picked = returned[position].reshape(tok_dev, TOPK, width).astype(jnp.float32)
    mixed = jnp.sum(route_weights[:, :, None] * picked, axis=1).astype(jnp.bfloat16)
    total = jnp.float32(tok_dev * devices)
    balance_loss = (
        jnp.sum(counts_all * sums_all) * jnp.float32(experts) / (jnp.float32(TOPK) * total * total)
    )
    return (mixed, balance_loss)


def solution(mesh):
    placed = (
        P(("node", "local"), None),
        P(("node", "local"), None),
        P(("node", "local"), None),
        P(("node", "local"), None, None),
        P(("node", "local"), None, None),
        P(("node", "local"), None, None),
    )
    return jax.shard_map(
        local,
        mesh=mesh,
        in_specs=placed,
        out_specs=(P(("node", "local"), None), P()),
        check_vma=False,
    )
```

profile of v0, /device:TPU:0, one launch (start us, length us, event | category | flops | bytes accessed | tf_op | source)
XLA Modules:
  0.0 619.0 jit_solution(2982418131425307916)
XLA Ops:
  0.6 0.8 copy.17
  1.4 0.1 eq.29
  1.6 0.1 eq.25
  1.7 0.7 broadcast_multiply_fusion
  2.4 1.7 reduce-window.6
  4.1 0.3 slice_reduce_fusion
  4.5 0.1 mul.53
  4.7 6.3 %broadcast_in_dim.5 = bf16[128,6,5120]{2,1,0:T(8,128)(2,1)} broadcast(bf16[128,5120]{1,0:T(8,128)(2,1)} %param.6), dimensions={0,2} | broadcast | bytes 9175040 | tf_op jit(solution)/shard_map/broadcast_in_dim | solution.py:36
  11.0 13.2 %reshape.127 = bf16[768,5120]{1,0:T(8,128)(2,1)} reshape(bf16[128,6,5120]{2,1,0:T(8,128)(2,1)} %broadcast_in_dim.5) | data formatting | bytes 15728640 | tf_op jit(solution)/shard_map/reshape | solution.py:36
  24.2 0.1 convert_reduce_fusion
  24.4 21.7 %scatter_custom_fusion = bf16[1024,5120]{1,0:T(8,128)(2,1)} fusion(s32[768]{0:T(1024)S(1)} %fusion.14, bf16[768,5120]{1,0:T(8,128)(2,1)} %reshape.127, bf16[]{:T(256)} %constant.7.clone.1), kind=kCustom, calls=%fused_computation.9 | custom fusion | bytes 10486272 | tf_op jit(solution)/shard_map/scatter | solution.py:37
  46.1 235.8 %all_to_all.8 = bf16[32,1,32,5120]{3,2,1,0:T(8,128)(2,1)S(1)} all-to-all(bf16[32,1,32,5120]{3,2,1,0:T(8,128)(2,1)} %bitcast.32), channel_id=1, replica_groups=mesh['node'=4,'local'=8] {'node','local'}, dimensions={0} | all-to-all | bytes 20971520 | tf_op jit(solution)/shard_map/all_to_all | solution.py:38
  281.9 10.9 %fusion.1 = f32[1024,768]{1,0:T(8,128)S(1)} fusion(bf16[1024,5120]{1,0:T(8,128)(2,1)S(1)} %bitcast.34, bf16[1,5120,768]{2,1,0:T(8,128)(2,1)} %param.10), kind=kOutput, calls=%fused_computation.5 | convolution fusion | flops 8053063680 | bytes 21495808 | tf_op jit(solution)/shard_map/erd,edf->erf/dot_general | solution.py:11
  292.8 8.6 %multiply_convert_fusion = bf16[1024,768]{1,0:T(8,128)(2,1)S(1)} fusion(f32[1024,768]{1,0:T(8,128)S(1)} %fusion.1, bf16[1024,5120]{1,0:T(8,128)(2,1)S(1)} %bitcast.35, bf16[1,5120,768]{2,1,0:T(8,128)(2,1)S(1)} %bitcast.38), kind=kOutput, calls=%fused_computation.11 | convolution fusion | flops 8057782272 | bytes 23068672 | tf_op jit(solution)/shard_map/erd,edf->erf/dot_general | solution.py:10
  301.4 13.7 %convolution_convert_fusion = bf16[1024,5120]{1,0:T(8,128)(2,1)} fusion(bf16[1024,768]{1,0:T(8,128)(2,1)S(1)} %multiply_convert_fusion, bf16[1,768,5120]{2,1,0:T(8,128)(2,1)} %param.11), kind=kOutput, calls=%fused_computation.3 | convolution fusion | flops 8058306560 | bytes 19922944 | tf_op jit(solution)/shard_map/erf,efd->erd/dot_general | solution.py:13
  315.1 3.9 all-to-all-start.1
  319.0 0.1 copy.15
  319.1 0.1 mul.58
  319.3 0.1 fusion.12
  319.4 250.9 %all-reduce = (f32[32]{0:T(128)S(1)}, f32[32]{0:T(128)S(1)}) all-reduce(f32[32]{0:T(128)S(1)} %convert_element_type.37, f32[32]{0:T(128)S(1)} %fusion.12), channel_id=1, replica_groups=mesh['node'=4,'local'=8] {'node','local'}, use_global_device_ids=true, to_apply=%region_6.7 | all-reduce | flops 64 | bytes 512 | tf_op jit(solution)/shard_map/psum | solution.py:35
  570.3 0.6 multiply_reduce_fusion.1
  571.6 20.0 %gather_fusion = bf16[768,5120]{1,0:T(8,128)(2,1)} fusion(bf16[1024,5120]{1,0:T(8,128)(2,1)} %bitcast.8, s32[1024]{0:T(1024)S(1)} %pad_clamp_fusion), kind=kCustom, calls=%fused_computation | custom fusion | bytes 15731712 | tf_op jit(solution)/shard_map/gather | solution.py:51
  591.6 14.3 %reshape.114 = f32[128,6,5120]{2,1,0:T(8,128)} reshape(bf16[768,5120]{1,0:T(8,128)(2,1)} %gather_fusion) | data formatting | bytes 23592960 | tf_op jit(solution)/shard_map/convert_element_type | solution.py:51
  605.9 12.0 %multiply_reduce_fusion = bf16[128,5120]{1,0:T(8,128)(2,1)} fusion(f32[128,6,5120]{2,1,0:T(8,128)} %reshape.114, f32[128,6]{1,0:T(8,128)S(1)} %copy.15), kind=kLoop, calls=%fused_computation.2 | loop fusion | flops 7208960 | bytes 17042432 | tf_op jit(solution)/shard_map/reduce_sum | solution.py:52
  (14 shorter events, 0.2 us)
Async XLA Ops:
  46.1 246.7 %slice-start = ((s8[7864320]{0:T(1024)(128)(4,1)}), s8[4194304]{0:T(1024)(128)(4,1)S(1)}, s32[]{:S(2)}) async-start(s8[7864320]{0:T(1024)(128)(4,1)} %bitcast.37), calls=%async_computation.2 | async-start | bytes 8388608
  281.9 10.9 %slice-start.1 = ((s8[7864320]{0:T(1024)(128)(4,1)}), s8[3670016]{0:T(1024)(128)(4,1)S(1)}, s32[]{:S(2)}) async-start(s8[7864320]{0:T(1024)(128)(4,1)} %bitcast.37), calls=%async_computation.3 | async-start | bytes 7340032
  315.1 3.9 copy-start
  315.1 256.4 %all-to-all-start.1 = ((bf16[1,32,32,5120]{3,2,0,1:T(8,128)(2,1)}), bf16[1,32,32,5120]{3,2,0,1:T(8,128)(2,1)}, u32[]{:S(2)}, u32[]{:S(2)}) async-start(bf16[1,32,32,5120]{3,2,0,1:T(8,128)(2,1)} %bitcast.33), calls=%async_computation.1 | async-start | bytes 20971520 | tf_op jit(solution)/shard_map/all_to_all | solution.py:49
where the time goes:
time: 620 us; the launch traced here: 619 us
  blocking collectives  487 us (79%)
  local copies, waits for them, and re-layouts  77.4 us (12%)
  matrix products  33.2 us (5%)
  other arithmetic  15.4 us (2%)
    psum x1, blocking collectives, local(): counts_all, sums_all = lax.psum((counts, weight_sums), ('node', 'local'))  251 us
    all_to_all x1, blocking collectives, local(): lax.all_to_all(outgoing.reshape(experts, 1, capacity, width), ('node', 'l...  236 us
    scatter x1, local copies, waits for them, and re-layouts, local(): jnp.zeros((experts * capacity, width), jnp.bfloat16).at[position]  21.7 us
    gather x1, local copies, waits for them, and re-layouts, local(): returned[position].reshape(tok_dev, TOPK, width).astype(jnp.float32)  20 us
    convert_element_type x1, local copies, waits for them, and re-layouts, local(): returned[position].reshape(tok_dev, TOPK, width).astype(jnp.float32)  14.3 us
    dot_general x1, matrix products, expert_apply(): jnp.einsum('erf,efd->erd', hidden, w_down, preferred_element_type=jnp.flo...  13.7 us
    reshape x1, local copies, waits for them, and re-layouts, local(): repeated = jnp.repeat(tokens, TOPK, axis=0)  13.2 us
  transfers between devices with their start and end apart: 1, of which 0 were waited for; matrix products, arithmetic and copies ran while one was open for 0% of the time, Pallas kernels for 0%

commit v1 on v0

--- a/solution.py
+++ b/solution.py
@@ -35,13 +35,11 @@
     counts_all, sums_all = lax.psum((counts, weight_sums), ("node", "local"))
     repeated = jnp.repeat(tokens, TOPK, axis=0)
     outgoing = jnp.zeros((experts * capacity, width), jnp.bfloat16).at[position].set(repeated)
-    piece = lax.all_to_all(
-        outgoing.reshape(experts, 1, capacity, width),
-        ("node", "local"),
-        split_axis=0,
-        concat_axis=1,
-        tiled=True,
-    )
+    part = outgoing.reshape(experts, 1, capacity, width)
+    count_2 = lax.axis_size(("node", "local"))
+    tiles = jnp.stack(jnp.split(part, count_2, axis=0), axis=0)
+    tiles = lax.all_to_all(tiles, ("node", "local"), split_axis=0, concat_axis=0)
+    piece = jnp.concatenate(tiles, axis=1)
     held, sources, count, breadth = piece.shape
     rows = piece.reshape(held, sources * count, breadth)
     result = expert_apply(rows, w_gate, w_up, w_down)

time: 620 us -> 650 us (1.048)
  local copies, waits for them, and re-layouts: 77.4 us -> 110 us
    unnamed x8 -> x43, local copies, waits for them, and re-layouts: 0.92 us -> 32 us
where the time goes in v1:
time: 650 us; the launch traced here: 648 us
  blocking collectives  486 us (75%)
  local copies, waits for them, and re-layouts  110 us (17%)
  matrix products  29.7 us (5%)
  other arithmetic  15.4 us (2%)
    psum x1, blocking collectives, local(): counts_all, sums_all = lax.psum((counts, weight_sums), ('node', 'local'))  251 us
    all_to_all x1, blocking collectives, local(): lax.all_to_all(tiles, ('node', 'local'), split_axis=0, concat_axis=0)  236 us
    unnamed x43, local copies, waits for them, and re-layouts  32 us
    scatter x1, local copies, waits for them, and re-layouts, local(): jnp.zeros((experts * capacity, width), jnp.bfloat16).at[position]  21.7 us
    gather x1, local copies, waits for them, and re-layouts, local(): returned[position].reshape(tok_dev, TOPK, width).astype(jnp.float32)  20 us
    convert_element_type x1, local copies, waits for them, and re-layouts, local(): returned[position].reshape(tok_dev, TOPK, width).astype(jnp.float32)  14.3 us
    reshape x1, local copies, waits for them, and re-layouts, local(): repeated = jnp.repeat(tokens, TOPK, axis=0)  13.2 us
  transfers between devices with their start and end apart: 1, of which 0 were waited for; matrix products, arithmetic and copies ran while one was open for 0% of the time, Pallas kernels for 0%

profile of v1, /device:TPU:0, one launch (start us, length us, event | category | flops | bytes accessed | tf_op | source)
XLA Modules:
  0.0 647.8 jit_solution(13282105609958515353)
XLA Ops:
  2.4 1.7 reduce-window.6
  4.7 6.3 broadcast_in_dim.5
  11.0 13.2 %reshape.183 = bf16[768,5120]{1,0:T(8,128)(2,1)} reshape(bf16[128,6,5120]{2,1,0:T(8,128)(2,1)} %broadcast_in_dim.5) | data formatting | bytes 15728640 | tf_op jit(solution)/shard_map/reshape | solution.py:36
  24.4 21.7 %scatter_custom_fusion = bf16[1024,5120]{1,0:T(8,128)(2,1)} fusion(s32[768]{0:T(1024)S(1)} %fusion.46, bf16[768,5120]{1,0:T(8,128)(2,1)} %reshape.183, bf16[]{:T(256)} %constant.7.clone.1), kind=kCustom, calls=%fused_computation.9 | custom fusion | bytes 10486272 | tf_op jit(solution)/shard_map/scatter | solution.py:37
  47.1 1.0 fusion.39
  48.1 1.0 fusion.38
  49.1 1.0 fusion.37
  50.1 1.0 fusion.36
  51.1 1.0 fusion.35
  52.1 1.0 fusion.34
  53.1 1.0 fusion.33
  54.1 1.0 fusion.32
  55.1 1.0 fusion.31
  76.1 1.1 fusion.10
  77.3 1.2 fusion.9
  78.5 235.6 %all_to_all.14 = bf16[32,1,1,32,5120]{4,3,2,1,0:T(8,128)(2,1)S(1)} all-to-all(bf16[32,1,1,32,5120]{4,3,2,1,0:T(8,128)(2,1)S(1)} %fusion.9), channel_id=1, replica_groups=mesh['node'=4,'local'=8] {'node','local'}, dimensions={0} | all-to-all | bytes 20971520 | tf_op jit(solution)/shard_map/all_to_all | solution.py:41
  314.1 8.3 %fusion.1 = f32[1024,768]{1,0:T(8,128)S(1)} fusion(bf16[1024,5120]{1,0:T(8,128)(2,1)S(1)} %bitcast.160, bf16[1,5120,768]{2,1,0:T(8,128)(2,1)S(1)} %bitcast.164), kind=kOutput, calls=%fused_computation.5 | convolution fusion | flops 8053063680 | bytes 21495808 | tf_op jit(solution)/shard_map/erd,edf->erf/dot_general | solution.py:11
  322.4 10.7 %multiply_convert_fusion = bf16[1024,768]{1,0:T(8,128)(2,1)S(1)} fusion(f32[1024,768]{1,0:T(8,128)S(1)} %fusion.1, bf16[1024,5120]{1,0:T(8,128)(2,1)S(1)} %bitcast.161, bf16[1,5120,768]{2,1,0:T(8,128)(2,1)} %param.9), kind=kOutput, calls=%fused_computation.11 | convolution fusion | flops 8057782272 | bytes 23068672 | tf_op jit(solution)/shard_map/erd,edf->erf/dot_general | solution.py:10
  333.1 10.7 %convolution_convert_fusion = bf16[1024,5120]{1,0:T(8,128)(2,1)} fusion(bf16[1024,768]{1,0:T(8,128)(2,1)S(1)} %multiply_convert_fusion, bf16[1,768,5120]{2,1,0:T(8,128)(2,1)S(1)} %bitcast.166), kind=kOutput, calls=%fused_computation.3 | convolution fusion | flops 8058306560 | bytes 19922944 | tf_op jit(solution)/shard_map/erf,efd->erd/dot_general | solution.py:13
  343.9 3.9 all-to-all-start.1
  348.1 250.9 %all-reduce = (f32[32]{0:T(128)S(1)}, f32[32]{0:T(128)S(1)}) all-reduce(f32[32]{0:T(128)S(1)} %convert_element_type.37, f32[32]{0:T(128)S(1)} %fusion.44), channel_id=1, replica_groups=mesh['node'=4,'local'=8] {'node','local'}, use_global_device_ids=true, to_apply=%region_6.7 | all-reduce | flops 64 | bytes 512 | tf_op jit(solution)/shard_map/psum | solution.py:35
  600.3 20.0 %gather_fusion = bf16[768,5120]{1,0:T(8,128)(2,1)} fusion(bf16[1024,5120]{1,0:T(8,128)(2,1)} %bitcast.39, s32[1024]{0:T(1024)S(1)} %pad_clamp_fusion), kind=kCustom, calls=%fused_computation | custom fusion | bytes 15731712 | tf_op jit(solution)/shard_map/gather | solution.py:49
  620.3 14.3 %reshape.170 = f32[128,6,5120]{2,1,0:T(8,128)} reshape(bf16[768,5120]{1,0:T(8,128)(2,1)} %gather_fusion) | data formatting | bytes 23592960 | tf_op jit(solution)/shard_map/convert_element_type | solution.py:49
  634.6 12.0 %multiply_reduce_fusion = bf16[128,5120]{1,0:T(8,128)(2,1)} fusion(f32[128,6,5120]{2,1,0:T(8,128)} %reshape.170, f32[128,6]{1,0:T(8,128)S(1)} %copy.15), kind=kLoop, calls=%fused_computation.2 | loop fusion | flops 7208960 | bytes 17042432 | tf_op jit(solution)/shard_map/reduce_sum | solution.py:50
  (51 shorter events, 24.4 us)
Async XLA Ops:
  76.1 238.0 %slice-start = ((s8[7864320]{0:T(1024)(128)(4,1)}), s8[4194304]{0:T(1024)(128)(4,1)S(1)}, s32[]{:S(2)}) async-start(s8[7864320]{0:T(1024)(128)(4,1)} %bitcast.163), calls=%async_computation.2 | async-start | bytes 8388608
  78.5 235.6 %slice-start.1 = ((s8[7864320]{0:T(1024)(128)(4,1)}), s8[3670016]{0:T(1024)(128)(4,1)S(1)}, s32[]{:S(2)}) async-start(s8[7864320]{0:T(1024)(128)(4,1)} %bitcast.163), calls=%async_computation.3 | async-start | bytes 7340032
  314.1 19.1 %slice-start.2 = ((s8[7864320]{0:T(1024)(128)(4,1)}), s8[3670016]{0:T(1024)(128)(4,1)S(1)}, s32[]{:S(2)}) async-start(s8[7864320]{0:T(1024)(128)(4,1)} %bitcast.165), calls=%async_computation.4 | async-start | bytes 7340032
  322.3 10.8 %slice-start.3 = ((s8[7864320]{0:T(1024)(128)(4,1)}), s8[4194304]{0:T(1024)(128)(4,1)S(1)}, s32[]{:S(2)}) async-start(s8[7864320]{0:T(1024)(128)(4,1)} %bitcast.165), calls=%async_computation.5 | async-start | bytes 8388608
  343.9 3.9 copy-start
  343.9 256.4 %all-to-all-start.1 = ((bf16[1,32,32,5120]{3,2,0,1:T(8,128)(2,1)}), bf16[1,32,32,5120]{3,2,0,1:T(8,128)(2,1)}, u32[]{:S(2)}, u32[]{:S(2)}) async-start(bf16[1,32,32,5120]{3,2,0,1:T(8,128)(2,1)} %bitcast.159), calls=%async_computation.1 | async-start | bytes 20971520 | tf_op jit(solution)/shard_map/all_to_all | solution.py:47
